TPU v7x, 32 devices: a whole 2x2x4 slice. The times are simulated.
32 devices in a mesh: lat: 4 (over z), lon: 8 (over y, x, core).
Axes of the slice: x: 2, y: 2, z: 4, core: 2. Of those that a mesh axis runs over, the one named last changes fastest.
Arguments:
- state: float32 [2, 3072, 6144], P(None, 'lat', 'lon'), may hold values from -6 to 6
- direction: float32 [2, 3072, 6144], P(None, 'lat', 'lon'), may hold values from -6 to 6
- diffusivity: bfloat16 [3072, 6144], P('lat', 'lon'), may hold values from 0.29882812 to 3
- inverses: bfloat16 [384, 8, 8, 12, 256], P(('lat', 'lon')), may hold values from -1.5 to 3
Outputs:
- preconditioned: float32 [2, 3072, 6144], P(None, 'lat', 'lon')
- jacobian_product: float32 [2, 3072, 6144], P(None, 'lat', 'lon')
All inputs are finite; a program needn't handle non-finite values.
Results may differ from a plain program's by a relative error of at most 0.0003.
Values sent between devices are 32-bit elements; how exact they have to be, the bound alone decides.
No kernel may reach another device: no remote copies, remote signals or barrier semaphores. Data moves between devices by JAX's collectives and lax.ppermute only.
A program may use at most 128 MiB of HBM per device.

v0:
```python
import jax
import jax.numpy as jnp
from jax import lax
from jax.sharding import PartitionSpec as P

zonal_tau = 0.1
merid_tau = 0.5
zonal_cap = 16.0
quad_coef = 0.25
step_size = 0.01
highest = lax.Precision.HIGHEST


def padded_2(block, sides, width):
    for axis, dim in sides:
        count = lax.axis_size(axis)
        forward = [(i, i + 1) for i in range(count - 1)]
        forward.append((count - 1, 0))
        backward = [(target, source) for source, target in forward]
        low = lax.ppermute(
            lax.slice_in_dim(block, block.shape[dim] - width, None, axis=dim), axis, forward
        )
        high = lax.ppermute(lax.slice_in_dim(block, 0, width, axis=dim), axis, backward)
        block = jnp.concatenate([low, block, high], axis=dim)
    return block


def lat_geometry(first_row, count, total):
    rows = (first_row + jnp.arange(count, dtype=jnp.int32)).astype(jnp.float32)
    limit = jnp.float32(total)
    cell_cos = jnp.sin(jnp.pi * (rows + 0.5) / limit)
    high_face = rows + 1.0
    face_low = jnp.where((rows > 0.0) & (rows < limit), jnp.sin(jnp.pi * rows / limit), 0.0)
    face_high = jnp.where(high_face < limit, jnp.sin(jnp.pi * high_face / limit), 0.0)
    zonal_factor = jnp.minimum(1.0 / (cell_cos * cell_cos), zonal_cap)
    return (cell_cos[:, None], face_low[:, None], face_high[:, None], zonal_factor[:, None])


def tendency(padded, kappa_field, cell_cos, face_low, face_high, zonal_factor):
    centre = padded[:, 1:-1, 1:-1]
    east_cell = padded[:, 1:-1, 2:]
    west_cell = padded[:, 1:-1, :-2]
    north_cell = padded[:, 2:, 1:-1]
    south_cell = padded[:, :-2, 1:-1]
    east_flux = (
        zonal_tau
        * zonal_factor
        * (1.0 + quad_coef * jnp.square(0.5 * (centre + east_cell)))
        * (east_cell - centre)
    )
    west_flux = (
        zonal_tau
        * zonal_factor
        * (1.0 + quad_coef * jnp.square(0.5 * (centre + west_cell)))
        * (centre - west_cell)
    )
    north_flux = (
        merid_tau
        * face_high
        * (1.0 + quad_coef * jnp.square(0.5 * (centre + north_cell)))
        * (north_cell - centre)
    )
    south_flux = (
        merid_tau
        * face_low
        * (1.0 + quad_coef * jnp.square(0.5 * (centre + south_cell)))
        * (centre - south_cell)
    )
    spread = east_flux - west_flux + (north_flux - south_flux) / cell_cos
    return centre - kappa_field * spread


def batch_apply(table, values):
    batch = values.shape[0]
    wide = jnp.broadcast_to(table, (batch,) + table.shape)
    return lax.dot_general(wide, values, (((2,), (1,)), ((0,), (0,))), precision=highest)


def solve_rows(pencil, inverses):
    items = pencil.shape[0]
    row_count = pencil.shape[1]
    block_rows = inverses.shape[1]
    outer = inverses.shape[3]
    half_inner = inverses.shape[4]
    inner = 2 * half_inner
    length = outer * inner
    outer_ids = jnp.arange(outer, dtype=jnp.int32)
    inner_ids = jnp.arange(inner, dtype=jnp.int32)
    half_ids = jnp.arange(half_inner, dtype=jnp.int32)
    outer_angle = (
        2.0 * jnp.pi * (outer_ids[:, None] * outer_ids[None, :] % outer).astype(jnp.float32) / outer
    )
    outer_cos = jnp.cos(outer_angle)
    outer_sin = jnp.sin(outer_angle)
    twist = (
        2.0
        * jnp.pi
        * (outer_ids[:, None] * inner_ids[None, :] % length).astype(jnp.float32)
        / length
    )
    twist_cos = jnp.cos(twist)
    twist_sin = jnp.sin(twist)
    inner_angle = (
        2.0 * jnp.pi * (inner_ids[:, None] * half_ids[None, :] % inner).astype(jnp.float32) / inner
    )
    inner_cos = jnp.cos(inner_angle)
    inner_sin = jnp.sin(inner_angle)
    forward_table = jnp.concatenate(
        [jnp.concatenate([inner_cos, -inner_sin], 1), jnp.concatenate([inner_sin, inner_cos], 1)], 0
    )
    inverse_table = jnp.concatenate(
        [
            jnp.concatenate([inner_cos.T, inner_sin.T], 1),
            jnp.concatenate([-inner_sin.T, inner_cos.T], 1),
        ],
        0,
    )
    weights = (
        jnp.where((outer_ids[:, None] == 0) & (half_ids[None, :] == 0), 1.0, 2.0).astype(
            jnp.float32
        )
        / length
    )
    grid = pencil.reshape(items * row_count, outer, inner)
    first_re = batch_apply(outer_cos, grid)
    first_im = -batch_apply(outer_sin, grid)
    turned_re = first_re * twist_cos + first_im * twist_sin
    turned_im = first_im * twist_cos - first_re * twist_sin
    spectrum = jnp.dot(jnp.concatenate([turned_re, turned_im], 2), forward_table, precision=highest)
    shape = (items, row_count // block_rows, block_rows, outer, half_inner)
    spec_re = spectrum[..., :half_inner].reshape(shape)
    spec_im = spectrum[..., half_inner:].reshape(shape)
    blocks = inverses.astype(jnp.float32)[None]
    solved_re = jnp.zeros(shape, jnp.float32)
    solved_im = jnp.zeros(shape, jnp.float32)
    for column in range(block_rows):
        factor = blocks[:, :, :, column]
        solved_re = solved_re + factor * spec_re[:, :, column][:, :, None]
        solved_im = solved_im + factor * spec_im[:, :, column][:, :, None]
    solved_re = (solved_re * weights).reshape(items * row_count, outer, half_inner)
    solved_im = (solved_im * weights).reshape(items * row_count, outer, half_inner)
    back = jnp.dot(jnp.concatenate([solved_re, solved_im], 2), inverse_table, precision=highest)
    back_re = back[..., :inner]
    back_im = back[..., inner:]
    rotated_re = back_re * twist_cos - back_im * twist_sin
    rotated_im = back_re * twist_sin + back_im * twist_cos
    values = batch_apply(outer_cos.T, rotated_re) - batch_apply(outer_sin.T, rotated_im)
    return values.reshape(items, row_count, length)


def spectral(direction, inverses):
    pencil = lax.all_to_all(direction, "lon", split_axis=1, concat_axis=2, tiled=True)
    values = solve_rows(pencil, inverses)
    return lax.all_to_all(values, "lon", split_axis=2, concat_axis=1, tiled=True)


def on_device(state, direction, diffusivity, inverses):
    local_rows = state.shape[1]
    state_pad = padded_2(state, (("lat", 1), ("lon", 2)), 1)
    preconditioned = spectral(direction, inverses)
    field_pad = padded_2(preconditioned, (("lat", 1), ("lon", 2)), 1)
    geometry = lat_geometry(
        lax.axis_index("lat") * local_rows, local_rows, lax.axis_size("lat") * local_rows
    )
    kappa_field = diffusivity.astype(jnp.float32)
    base = tendency(state_pad, kappa_field, *geometry)
    moved = tendency(state_pad + step_size * field_pad, kappa_field, *geometry)
    jacobian_product = (moved - base) / step_size
    return (preconditioned, jacobian_product)


def solution(mesh):
    return jax.shard_map(
        on_device,
        mesh=mesh,
        in_specs=(
            P(None, "lat", "lon"),
            P(None, "lat", "lon"),
            P("lat", "lon"),
            P(("lat", "lon"), None, None, None, None),
        ),
        out_specs=(P(None, "lat", "lon"), P(None, "lat", "lon")),
        check_vma=False,
    )
```

profile of v0, /device:TPU:0, one launch (start us, length us, event | category | flops | bytes accessed | tf_op | source)
XLA Modules:
  0.0 356.4 jit_solution(17344552827916341534)
XLA Ops:
  0.6 8.2 %copy.189 = f32[2,768,768]{2,0,1:T(2,128)} copy(f32[2,768,768]{2,1,0:T(8,128)} %param.5) | data formatting | bytes 9437184 | tf_op args[1]
  8.8 5.5 %all-to-all-start = ((f32[2,768,768]{2,0,1:T(2,128)}), f32[2,768,768]{2,0,1:T(2,128)}, u32[]{:S(2)}, u32[]{:S(2)}) async-start(f32[2,768,768]{2,0,1:T(2,128)} %copy.189), calls=%async_computation | async-start | bytes 9437184 | tf_op jit(solution)/shard_map/all_to_all | solution.py:152
  14.4 0.8 fusion.95
  15.2 2.7 fusion.89
  17.9 2.7 fusion.90
  20.5 2.9 fusion.87
  23.4 2.9 fusion.85
  26.3 0.7 select_multiply_fusion
  27.0 5.8 %bitcast_convert_fusion = f32[1,12,8,8,12,256]{5,2,4,3,1,0:T(8,128)S(1)} fusion(bf16[12,8,8,12,256]{4,2,3,1,0:T(8,128)(2,1)} %param.7), kind=kLoop, calls=%fused_computation.63 | loop fusion | flops 2359296 | bytes 14155776 | tf_op jit(solution)/shard_map/broadcast_in_dim | solution.py:133
  32.8 2.8 slice_bitcast_fusion.7
  35.6 33.5 %all-to-all-done = f32[2,768,768]{2,0,1:T(2,128)} async-done(((f32[2,768,768]{2,0,1:T(2,128)}), f32[2,768,768]{2,0,1:T(2,128)}, u32[]{:S(2)}, u32[]{:S(2)}) %all-to-all-start) | async-done | bytes 4718624 | tf_op jit(solution)/shard_map/all_to_all | solution.py:152
  69.0 7.3 %copy.338 = f32[2,8,96,768]{3,1,2,0:T(8,128)} copy(f32[2,8,96,768]{3,0,2,1:T(2,128)} %bitcast.2) | data formatting | bytes 9437184 | tf_op jit(solution)/shard_map/all_to_all | solution.py:152
  76.3 7.3 %reshape.189 = f32[192,12,512]{2,1,0:T(8,128)} reshape(f32[2,96,8,768]{3,2,1,0:T(8,128)} %bitcast.98) | data formatting | bytes 9437184 | tf_op jit(solution)/shard_map/reshape | solution.py:124
  83.6 7.8 %fusion.68 = f32[192,12,512]{2,1,0:T(8,128)S(1)} fusion(f32[192,12,512]{2,1,0:T(8,128)} %reshape.189, f32[12,12]{1,0:T(8,128)S(1)} %fusion.102), kind=kOutput, calls=%fused_computation.110 | convolution fusion | flops 169869312 | bytes 9437760 | tf_op jit(solution)/shard_map/dot_general | solution.py:76
  91.5 9.4 %multiply_add_fusion = (f32[192,12,512]{2,1,0:T(8,128)}, f32[192,12,512]{2,1,0:T(8,128)}) fusion(f32[192,12,512]{2,1,0:T(8,128)S(1)} %fusion.68, f32[12,512]{1,0:T(8,128)S(1)} %copy-done.11, f32[12,512]{1,0:T(8,128)S(1)} %copy-done.13, f32[192,12,512]{2,1,0:T(8,128)S(1)} %copy-done, f32[12,12]{1,0:T(8,128)S(1)} %fusion.103), kind=kOutput, calls=%fused_computation.12 | convolution fusion | flops 178126848 | bytes 18924096 | tf_op jit(solution)/shard_map/dot_general | solution.py:76
  100.9 11.8 %pad_maximum_fusion = f32[192,12,1024]{2,1,0:T(8,128)} fusion(f32[192,12,512]{2,1,0:T(8,128)} %get-tuple-element.5, f32[192,12,512]{2,1,0:T(8,128)} %get-tuple-element.4), kind=kLoop, calls=%fused_computation | loop fusion | flops 2359296 | bytes 18874368 | tf_op jit(solution)/shard_map/concatenate | solution.py:129
  112.6 24.9 %fusion = f32[192,12,512]{2,0,1:T(8,128)S(1)} fusion(f32[192,12,1024]{2,1,0:T(8,128)} %pad_maximum_fusion, f32[512,256]{1,0:T(8,128)} %get-tuple-element.47, f32[512,256]{1,0:T(8,128)} %get-tuple-element.46, f32[512,256]{1,0:T(8,128)} %fusion.89), kind=kOutput, calls=%fused_computation.1 | convolution fusion | flops 14497087488 | bytes 15728640 | tf_op jit(solution)/shard_map/dot_general | solution.py:129
  137.6 0.6 fusion.112
  138.2 1.6 fusion.114
  142.0 1.6 fusion.113
  146.5 3.3 add_add_fusion
  149.9 3.8 %add_add_fusion.1 = f32[2,12,8,12,256]{4,2,1,0,3:T(8,128)S(1)} fusion(f32[2,12,12,256]{3,1,0,2:T(8,128)S(1)} %copy.214, f32[2,12,12,256]{3,1,0,2:T(8,128)S(1)} %copy.211, f32[2,12,12,256]{3,1,0,2:T(8,128)S(1)} %copy.208, f32[2,12,12,256]{3,1,0,2:T(8,128)S(1)} %copy.205, f32[2,12,12,256]{3,1,0,2:T(8,128)S(1)} %copy.202, f32[2,12,12,256]{3,1,0,2:T(8,128)S(1)} %copy.199, ...), kind=kLoop, calls=%fused_computation.74 | loop fusion | flops 8847360 | bytes 14155776 | tf_op jit(solution)/shard_map/add | solution.py:138
  155.0 16.8 %fusion.44 = f32[192,12,1024]{2,0,1:T(8,128)S(1)} fusion(f32[192,12,256]{2,0,1:T(8,128)S(1)} %get-tuple-element.43, f32[192,12,256]{2,0,1:T(8,128)S(1)} %get-tuple-element.42, f32[256,512]{1,0:T(8,128)S(1)} %copy-done.10, f32[256,512]{1,0:T(8,128)S(1)} %copy-done.8, f32[256,512]{1,0:T(8,128)S(1)} %copy-done.9), kind=kOutput, calls=%fused_computation.59 | convolution fusion | flops 14498267136 | bytes 15728640 | tf_op jit(solution)/shard_map/dot_general | solution.py:142
  171.8 1.6 fusion.109
  173.5 12.0 %fusion.3 = f32[192,12,512]{2,1,0:T(8,128)S(1)} fusion(f32[192,12,512]{2,0,1:T(8,128)S(1)} %get-tuple-element.7, f32[192,12,512]{2,0,1:T(8,128)S(1)} %get-tuple-element.6, f32[12,512]{1,0:T(8,128)S(1)} %copy-done.12, f32[12,512]{1,0:T(8,128)S(1)} %copy-done.14, f32[12,12]{1,0:T(8,128)S(1)} %fusion.103), kind=kOutput, calls=%fused_computation.8 | convolution fusion | flops 173408256 | bytes 14205504 | tf_op jit(solution)/shard_map/dot_general | solution.py:76
  185.5 14.6 %fusion.52 = f32[192,12,512]{2,1,0:T(8,128)} fusion(f32[192,12,512]{2,1,0:T(8,128)S(1)} %fusion.3, f32[192,12,512]{2,0,1:T(8,128)S(1)} %get-tuple-element.7, f32[192,12,512]{2,0,1:T(8,128)S(1)} %get-tuple-element.6, f32[12,512]{1,0:T(8,128)S(1)} %copy-done.12, f32[12,512]{1,0:T(8,128)S(1)} %copy-done.14, f32[12,12]{1,0:T(8,128)S(1)} %fusion.102), kind=kOutput, calls=%fused_computation.70 | convolution fusion | flops 174587904 | bytes 18924096 | tf_op jit(solution)/shard_map/dot_general | solution.py:76
  200.1 7.0 %reshape.192 = f32[2,96,6144]{2,1,0:T(8,128)} reshape(f32[192,12,512]{2,1,0:T(8,128)} %fusion.52) | data formatting | bytes 9437184 | tf_op jit(solution)/shard_map/reshape | solution.py:148
  207.1 8.9 %copy.233 = f32[2,96,6144]{1,0,2:T(2,128)} copy(f32[2,96,6144]{2,1,0:T(8,128)} %reshape.192) | data formatting | bytes 9437184 | tf_op jit(solution)/shard_map/reshape | solution.py:148
  216.0 4.8 %all-to-all-start.1 = ((f32[2,96,6144]{1,0,2:T(2,128)}), f32[2,96,6144]{1,0,2:T(2,128)}, u32[]{:S(2)}, u32[]{:S(2)}) async-start(f32[2,96,6144]{1,0,2:T(2,128)} %copy.233), calls=%async_computation.1 | async-start | bytes 12582912 | tf_op jit(solution)/shard_map/all_to_all | solution.py:154
  220.8 0.8 fusion.111
  221.7 2.4 collective-permute-start
  224.0 2.3 collective-permute-start.1
  226.5 65.9 %all-to-all-done.1 = f32[2,96,6144]{1,0,2:T(2,128)} async-done(((f32[2,96,6144]{1,0,2:T(2,128)}), f32[2,96,6144]{1,0,2:T(2,128)}, u32[]{:S(2)}, u32[]{:S(2)}) %all-to-all-start.1) | async-done | bytes 4718624 | tf_op jit(solution)/shard_map/all_to_all | solution.py:154
  292.4 9.8 %copy.247 = f32[2,96,8,768]{3,1,2,0:T(8,128)} copy(f32[2,96,8,768]{1,0,3,2:T(2,128)} %bitcast.34) | data formatting | bytes 9437184 | tf_op jit(solution)/shard_map/all_to_all | solution.py:154
  302.2 0.8 fusion.110
  303.0 2.4 collective-permute-start.4
  305.4 2.1 collective-permute-start.5
  307.5 1.7 pad_maximum_fusion.14
  309.9 2.7 collective-permute-start.3
  312.5 1.7 pad_maximum_fusion.11
  314.9 2.7 collective-permute-start.7
  317.6 1.5 convert_element_type.81
  319.1 1.2 copy.238
  320.3 1.2 copy.239
  321.5 1.2 copy.242
  322.7 1.2 copy.243
  323.9 9.1 %maximum_add_fusion = f32[2,770,770]{2,1,0:T(8,128)S(1)} fusion(f32[2,770,1]{2,1,0:T(8,128)} %copy.239, f32[2,1,768]{2,1,0:T(1,128)S(1)} %collective-permute-done.1, f32[2,768,768]{2,1,0:T(8,128)} %param.4, f32[2,1,768]{2,1,0:T(1,128)S(1)} %collective-permute-done, f32[2,770,1]{2,1,0:T(8,128)} %copy.238, f32[2,770,1]{2,1,0:T(8,128)} %copy.243, ...), kind=kLoop, calls=%fused_computation.13 | loop fusion | flops 11858000 | bytes 14229600 | tf_op jit(solution)/shard_map/add | solution.py:167
  333.0 22.9 %subtract_multiply_fusion = f32[2,768,768]{2,1,0:T(8,128)} fusion(f32[2,768,768]{2,1,0:T(8,128)S(1)} %bitcast.93, f32[2,770,770]{2,1,0:T(8,128)S(1)} %maximum_add_fusion, f32[2,1,768]{2,1,0:T(1,128)S(1)} %collective-permute-done, f32[2,1,768]{2,1,0:T(1,128)S(1)} %collective-permute-done.1, f32[2,770,1]{2,1,0:T(8,128)S(1)} %copy-done.6, ...), kind=kLoop, calls=%fused_computation.65 | loop fusion | flops 101449728 | bytes 35426336 | tf_op jit(solution)/shard_map/div | solution.py:168
  (90 shorter events, 7.6 us)
Async XLA Ops:
  8.8 60.2 %all-to-all-start = ((f32[2,768,768]{2,0,1:T(2,128)}), f32[2,768,768]{2,0,1:T(2,128)}, u32[]{:S(2)}, u32[]{:S(2)}) async-start(f32[2,768,768]{2,0,1:T(2,128)} %copy.189), calls=%async_computation | async-start | bytes 9437184 | tf_op jit(solution)/shard_map/all_to_all | solution.py:152
  83.6 7.9 %copy-start = (f32[192,12,512]{2,1,0:T(8,128)S(1)}, f32[192,12,512]{2,1,0:T(8,128)}, u32[]{:S(2)}) copy-start(f32[192,12,512]{2,1,0:T(8,128)} %reshape.189) | copy-start | bytes 14155780
  83.6 7.9 %copy-start.11 = (f32[12,512]{1,0:T(8,128)S(1)}, f32[12,512]{1,0:T(8,128)}, u32[]{:S(2)}) copy-start(f32[12,512]{1,0:T(8,128)} %get-tuple-element.44) | copy-start | bytes 73732
  83.6 7.9 %copy-start.13 = (f32[12,512]{1,0:T(8,128)S(1)}, f32[12,512]{1,0:T(8,128)}, u32[]{:S(2)}) copy-start(f32[12,512]{1,0:T(8,128)} %get-tuple-element.45) | copy-start | bytes 73732
  143.8 2.1 copy-start.1
  143.8 2.1 copy-start.2
  143.8 2.1 copy-start.3
  143.8 2.3 copy-start.4
  143.8 2.7 copy-start.5
  149.8 3.8 %copy-start.15 = (f32[12,256]{1,0:T(8,128)S(1)}, f32[12,256]{1,0:T(8,128)}, u32[]{:S(2)}) copy-start(f32[12,256]{1,0:T(8,128)} %select_multiply_fusion) | copy-start | bytes 36868
  153.7 1.0 copy-start.8
  153.7 1.2 copy-start.9
  153.7 1.3 copy-start.10
  171.8 1.7 copy-start.12
  171.8 1.7 copy-start.14
  216.0 76.3 %all-to-all-start.1 = ((f32[2,96,6144]{1,0,2:T(2,128)}), f32[2,96,6144]{1,0,2:T(2,128)}, u32[]{:S(2)}, u32[]{:S(2)}) async-start(f32[2,96,6144]{1,0,2:T(2,128)} %copy.233), calls=%async_computation.1 | async-start | bytes 12582912 | tf_op jit(solution)/shard_map/all_to_all | solution.py:154
  221.7 85.9 %collective-permute-start = (f32[2,1,768]{2,1,0:T(1,128)S(1)}, f32[2,1,768]{2,1,0:T(1,128)S(1)}, u32[]{:S(2)}, u32[]{:S(2)}) collective-permute-start(f32[2,1,768]{2,1,0:T(1,128)S(1)} %get-tuple-element.22), channel_id=1, source_target_pairs={{0,8},{8,16},{16,24},{24,0},{1,9},{9,17},{17,25},{25,1},{2,10},{10... | collective-permute-start | bytes 18440 | tf_op jit(solution)/shard_map/ppermute | solution.py:20
  224.0 83.5 %collective-permute-start.1 = (f32[2,1,768]{2,1,0:T(1,128)S(1)}, f32[2,1,768]{2,1,0:T(1,128)S(1)}, u32[]{:S(2)}, u32[]{:S(2)}) collective-permute-start(f32[2,1,768]{2,1,0:T(1,128)S(1)} %get-tuple-element.23), channel_id=1, source_target_pairs={{8,0},{16,8},{24,16},{0,24},{9,1},{17,9},{25,17},{1,25},{10,2},{18... | collective-permute-start | bytes 18440 | tf_op jit(solution)/shard_map/ppermute | solution.py:23
  303.0 9.5 %collective-permute-start.4 = (f32[2,1,768]{2,1,0:T(1,128)S(1)}, f32[2,1,768]{2,1,0:T(1,128)S(1)}, u32[]{:S(2)}, u32[]{:S(2)}) collective-permute-start(f32[2,1,768]{2,1,0:T(1,128)S(1)} %get-tuple-element.20), channel_id=1, source_target_pairs={{0,8},{8,16},{16,24},{24,0},{1,9},{9,17},{17,25},{25,1},{2,10},{10... | collective-permute-start | bytes 18440 | tf_op jit(solution)/shard_map/ppermute | solution.py:20
  305.4 7.1 %collective-permute-start.5 = (f32[2,1,768]{2,1,0:T(1,128)S(1)}, f32[2,1,768]{2,1,0:T(1,128)S(1)}, u32[]{:S(2)}, u32[]{:S(2)}) collective-permute-start(f32[2,1,768]{2,1,0:T(1,128)S(1)} %get-tuple-element.21), channel_id=1, source_target_pairs={{8,0},{16,8},{24,16},{0,24},{9,1},{17,9},{25,17},{1,25},{10,2},{18... | collective-permute-start | bytes 18440 | tf_op jit(solution)/shard_map/ppermute | solution.py:23
  309.5 9.5 %collective-permute-start.2 = (f32[2,770,1]{1,0,2:T(2,128)S(1)}, f32[2,770,1]{1,0,2:T(2,128)S(1)}, u32[]{:S(2)}, u32[]{:S(2)}) collective-permute-start(f32[2,770,1]{1,0,2:T(2,128)S(1)} %copy.236), channel_id=1, source_target_pairs={{0,1},{1,2},{2,3},{3,4},{4,5},{5,6},{6,7},{7,0},{8,9},{9,10},{10,1... | collective-permute-start | bytes 18488 | tf_op jit(solution)/shard_map/ppermute | solution.py:20
  309.9 10.4 %collective-permute-start.3 = (f32[2,770,1]{1,0,2:T(2,128)S(1)}, f32[2,770,1]{1,0,2:T(2,128)S(1)}, u32[]{:S(2)}, u32[]{:S(2)}) collective-permute-start(f32[2,770,1]{1,0,2:T(2,128)S(1)} %copy.237), channel_id=1, source_target_pairs={{1,0},{2,1},{3,2},{4,3},{5,4},{6,5},{7,6},{0,7},{9,8},{10,9},{11,1... | collective-permute-start | bytes 18488 | tf_op jit(solution)/shard_map/ppermute | solution.py:23
  314.5 7.0 %collective-permute-start.6 = (f32[2,770,1]{1,0,2:T(2,128)S(1)}, f32[2,770,1]{1,0,2:T(2,128)S(1)}, u32[]{:S(2)}, u32[]{:S(2)}) collective-permute-start(f32[2,770,1]{1,0,2:T(2,128)S(1)} %copy.240), channel_id=1, source_target_pairs={{0,1},{1,2},{2,3},{3,4},{4,5},{5,6},{6,7},{7,0},{8,9},{9,10},{10,1... | collective-permute-start | bytes 18488 | tf_op jit(solution)/shard_map/ppermute | solution.py:20
  314.9 7.9 %collective-permute-start.7 = (f32[2,770,1]{1,0,2:T(2,128)S(1)}, f32[2,770,1]{1,0,2:T(2,128)S(1)}, u32[]{:S(2)}, u32[]{:S(2)}) collective-permute-start(f32[2,770,1]{1,0,2:T(2,128)S(1)} %copy.241), channel_id=1, source_target_pairs={{1,0},{2,1},{3,2},{4,3},{5,4},{6,5},{7,6},{0,7},{9,8},{10,9},{11,1... | collective-permute-start | bytes 18488 | tf_op jit(solution)/shard_map/ppermute | solution.py:23
  317.6 15.4 %slice-start = ((s8[4718592]{0:T(1024)(128)(4,1)}), s8[524288]{0:T(1024)(128)(4,1)S(1)}, s32[]{:S(2)}) async-start(s8[4718592]{0:T(1024)(128)(4,1)} %bitcast.92), calls=%async_computation.2 | async-start | bytes 1048576
  323.9 9.1 %slice-start.1 = ((s8[4718592]{0:T(1024)(128)(4,1)}), s8[4194304]{0:T(1024)(128)(4,1)S(1)}, s32[]{:S(2)}) async-start(s8[4718592]{0:T(1024)(128)(4,1)} %bitcast.92), calls=%async_computation.3 | async-start | bytes 8388608
  323.9 9.1 %copy-start.6 = (f32[2,770,1]{2,1,0:T(8,128)S(1)}, f32[2,770,1]{2,1,0:T(8,128)}, u32[]{:S(2)}) copy-start(f32[2,770,1]{2,1,0:T(8,128)} %copy.238) | copy-start | bytes 18484
  323.9 9.1 %copy-start.7 = (f32[2,770,1]{2,1,0:T(8,128)S(1)}, f32[2,770,1]{2,1,0:T(8,128)}, u32[]{:S(2)}) copy-start(f32[2,770,1]{2,1,0:T(8,128)} %copy.239) | copy-start | bytes 18484
where the time goes:
time: 361 us; the launch traced here: 356 us
  waiting for transfers between devices  99.4 us (28%)
  matrix products  85.6 us (24%)
  other arithmetic  74.9 us (21%)
  local copies, waits for them, and re-layouts  69.9 us (19%)
  starting transfers between devices  24.8 us (7%)
    all_to_all x1, waiting for transfers between devices, spectral(): lax.all_to_all(values, 'lon', split_axis=2, concat_axis=1, tiled=True)  65.9 us
    dot_general x4, matrix products, batch_apply(): lax.dot_general(wide, values, (((2,), (1,)), ((0,), (0,))), precision=hig...  43.9 us
    all_to_all x1, waiting for transfers between devices, spectral(): lax.all_to_all(direction, 'lon', split_axis=1, concat_axis=2, tiled=True)  33.5 us
    dot_general x1, matrix products, solve_rows(): jnp.dot(jnp.concatenate([turned_re, turned_im], 2), forward_table, precis...  24.9 us
    div x1, other arithmetic, on_device(): jacobian_product = (moved - base) / step_size  22.9 us
    dot_general x1, matrix products, solve_rows(): jnp.dot(jnp.concatenate([solved_re, solved_im], 2), inverse_table, precis...  16.8 us
    reshape x2, local copies, waits for them, and re-layouts, solve_rows(): return values.reshape(items, row_count, length)  15.9 us
    unnamed x53, local copies, waits for them, and re-layouts  12.1 us
  transfers between devices with their start and end apart: 10, of which 2 were waited for; matrix products, arithmetic and copies ran while one was open for 12% of the time, Pallas kernels for 0%

commit v1 on v0

v1 whole, which is shorter than its diff:
```python
import functools
import math

import jax
import jax.numpy as jnp
from jax import lax
from jax.experimental import pallas as pl
from jax.experimental.pallas import tpu as pltpu
from jax.sharding import PartitionSpec as P


zonal_tau = 0.1
merid_tau = 0.5
zonal_cap = 16.0
step_size = 0.01


def scaled(value, factor):
    if value is None or abs(factor) < 1e-12:
        return None
    if abs(factor - 1.0) < 1e-12:
        return value
    if abs(factor + 1.0) < 1e-12:
        return -value
    return value * jnp.float32(factor)


def added(first, second, sign=1.0):
    if second is None:
        return first
    if first is None:
        return second if sign > 0 else -second
    return first + second if sign > 0 else first - second


def trig_sums(values, size, trig):
    sums = []
    for q in range(size // 4 + 1):
        parts = [None, None]
        groups = [{}, {}]
        for j, value in values:
            factor = trig(2.0 * math.pi * ((j * q) % size) / size)
            if abs(factor) < 1e-12:
                continue
            key = round(abs(factor), 9)
            total = groups[j % 2].get(key, (None, abs(factor)))[0]
            groups[j % 2][key] = (added(total, value, 1.0 if factor > 0 else -1.0), abs(factor))
        for parity in (0, 1):
            for total, factor in groups[parity].values():
                parts[parity] = added(parts[parity], scaled(total, factor))
        sums.append(parts)
    return sums


def real_outer(xs):
    size = len(xs)
    half = size // 2
    even = [(0, xs[0]), (half, xs[half])] + [(j, xs[j] + xs[size - j]) for j in range(1, half)]
    odd = [(j, xs[j] - xs[size - j]) for j in range(1, half)]
    re = [None] * (half + 1)
    im = [None] * (half + 1)
    for q, (a, b) in enumerate(trig_sums(even, size, math.cos)):
        re[q] = added(a, b)
        re[half - q] = added(a, b, -1.0)
    for q, (a, b) in enumerate(trig_sums(odd, size, math.sin)):
        total = added(a, b)
        im[q] = None if total is None else -total
        if q != half - q:
            im[half - q] = added(a, b, -1.0)
    return re, im


def real_outer_back(re, im, half):
    size = 2 * half
    xs = [None] * size
    cosines = trig_sums(list(enumerate(re)), size, math.cos)
    sines = trig_sums([(q, im[q]) for q in range(1, half)], size, math.sin)
    for j in range(size // 4 + 1):
        a, b = cosines[j]
        c, d = sines[j]
        even_part, odd_part = added(a, b), added(c, d)
        xs[j] = added(even_part, odd_part, -1.0)
        if j > 0:
            xs[size - j] = added(even_part, odd_part)
        even_part, odd_part = added(a, b, -1.0), added(d, c, -1.0)
        xs[half - j] = added(even_part, odd_part, -1.0)
        if j > 0:
            xs[half + j] = added(even_part, odd_part)
    return xs


def split_product(values, high, low):
    top = values.astype(jnp.bfloat16)
    rest = (values - top.astype(jnp.float32)).astype(jnp.bfloat16)
    dot = functools.partial(jnp.dot, preferred_element_type=jnp.float32)
    return dot(top, high) + (dot(rest, high) + dot(top, low))


def spectral_kernel(
    outer, inner, step_rows,
    y_ref, inv_ref, tc_ref, ts_ref, fh_ref, fl_ref, gh_ref, gl_ref,
    out_ref, z_ref, s_ref,
):
    half_inner = inner // 2
    half = outer // 2
    width = y_ref.shape[2]
    tile = math.gcd(math.gcd(inner, width), 256)
    groups = step_rows // 8
    step = pl.program_id(0)
    first = step * step_rows
    sources = y_ref.shape[0]
    share = out_ref.shape[1] - 8

    def place(j, h):
        n = j * inner + h * tile
        return n // width, n % width

    def forward(g, carry):
        rows = pl.ds(pl.multiple_of(g * 8, 8), 8)
        for h in range(inner // tile):
            cols = slice(h * tile, (h + 1) * tile)
            xs = []
            for j in range(outer):
                d, c = place(j, h)
                xs.append(y_ref[d, rows, c : c + tile])
            re, im = real_outer(xs)
            for q in range(outer):
                a, b = (re[q], im[q]) if q <= half else (re[outer - q], im[outer - q])
                if q > half and b is not None:
                    b = -b
                if q == 0:
                    zr, zi = a, jnp.zeros_like(a)
                else:
                    tc, ts = tc_ref[q, :, cols], ts_ref[q, :, cols]
                    if b is None:
                        zr, zi = a * tc, -(a * ts)
                    else:
                        zr, zi = a * tc + b * ts, b * tc - a * ts
                z_ref[q, rows, h * tile : (h + 1) * tile] = zr
                z_ref[q, rows, inner + h * tile : inner + (h + 1) * tile] = zi
        return carry

    lax.fori_loop(0, groups, forward, 0)
    flat = (outer * step_rows, 2 * inner)
    s_ref[...] = split_product(z_ref[...].reshape(flat), fh_ref[...], fl_ref[...]).reshape(s_ref.shape)

    lane = lax.broadcasted_iota(jnp.int32, (1, half_inner), 1)

    def solve(q, carry):
        weight = jnp.where((lane == 0) & (q == 0), 0.5, 1.0).astype(jnp.float32)
        for g in range(groups):
            re = im = None
            for s in range(8):
                factor = inv_ref[g, q, s].astype(jnp.float32)
                source = pl.ds(g * 8 + s, 8, stride=0)
                both = s_ref[q, source, :]
                sr, si = both[:, :half_inner], both[:, half_inner:]
                re = factor * sr if re is None else re + factor * sr
                im = factor * si if im is None else im + factor * si
            s_ref[q, g * 8 : g * 8 + 8, :half_inner] = re * weight
            s_ref[q, g * 8 : g * 8 + 8, half_inner:] = im * weight
        return carry

    lax.fori_loop(0, outer, solve, 0)
    flat = (outer * step_rows, 2 * half_inner)
    z_ref[...] = split_product(s_ref[...].reshape(flat), gh_ref[...], gl_ref[...]).reshape(z_ref.shape)

    def backward(g, carry):
        rows = pl.ds(pl.multiple_of(g * 8, 8), 8)
        target = pl.ds(pl.multiple_of(first + g * 8, 8), 8)
        for h in range(inner // tile):
            cols = slice(h * tile, (h + 1) * tile)

            def turned(q, want_im):
                ur = z_ref[q, rows, h * tile : (h + 1) * tile]
                if q == 0:
                    return ur, None
                ui = z_ref[q, rows, inner + h * tile : inner + (h + 1) * tile]
                tc, ts = tc_ref[q, :, cols], ts_ref[q, :, cols]
                return ur * tc - ui * ts, (ur * ts + ui * tc if want_im else None)

            re, im = [], []
            for q in range(half + 1):
                paired = 0 < q < half
                a, b = turned(q, paired)
                if paired:
                    c, d = turned(outer - q, True)
                    a, b = a + c, b - d
                re.append(a)
                im.append(b)
            for j, x in enumerate(real_outer_back(re, im, half)):
                d, c = place(j, h)
                out_ref[d, target, c : c + tile] = x
        return carry

    lax.fori_loop(0, groups, backward, 0)

    @pl.when(step == pl.num_programs(0) - 1)
    def _():
        for d in range(sources):
            here = slice(0, share)
            turned = jnp.transpose(out_ref[d, here, width - 128 :], (1, 0))
            out_ref[(d + 1) % sources, share : share + 1, here] = turned[127:128]
            turned = jnp.transpose(out_ref[d, here, :128], (1, 0))
            out_ref[(d - 1) % sources, share + 1 : share + 2, here] = turned[0:1]


def spectral(y, inverses, tables, step_rows):
    sources, row_count, width = y.shape
    outer = inverses.shape[1]
    inner = sources * width // outer
    half_inner = inverses.shape[4]
    block_rows = inverses.shape[2]
    whole = lambda array: pl.BlockSpec(array.shape, lambda i, n=array.ndim: (0,) * n)
    strip = pl.BlockSpec((sources, step_rows, width), lambda i: (0, i, 0))
    return pl.pallas_call(
        functools.partial(spectral_kernel, outer, inner, step_rows),
        grid=(row_count // step_rows,),
        in_specs=[
            strip,
            pl.BlockSpec(
                (step_rows // block_rows,) + inverses.shape[1:], lambda i: (i, 0, 0, 0, 0)
            ),
        ]
        + [whole(table) for table in tables],
        out_specs=pl.BlockSpec((sources, row_count + 8, width), lambda i: (0, 0, 0)),
        out_shape=jax.ShapeDtypeStruct((sources, row_count + 8, width), jnp.float32),
        scratch_shapes=[
            pltpu.VMEM((outer, step_rows, 2 * inner), jnp.float32),
            pltpu.VMEM((outer, step_rows, 2 * half_inner), jnp.float32),
        ],
        compiler_params=pltpu.CompilerParams(
            dimension_semantics=("arbitrary",), vmem_limit_bytes=36 * 1024 * 1024
        ),
        name="spectral",
    )(y, inverses, *tables)


def split_table(table):
    high = lax.reduce_precision(table, 8, 7)
    return high.astype(jnp.bfloat16), (table - high).astype(jnp.bfloat16)


def transform_tables(outer, inner):
    length = outer * inner
    half_inner = inner // 2
    outer_ids = jnp.arange(outer, dtype=jnp.int32)
    inner_ids = jnp.arange(inner, dtype=jnp.int32)
    half_ids = jnp.arange(half_inner, dtype=jnp.int32)
    twist = (
        2.0
        * jnp.pi
        * (outer_ids[:, None] * inner_ids[None, :] % length).astype(jnp.float32)
        / length
    )
    spread = lambda table: jnp.broadcast_to(table[:, None, :], (outer, 8, inner))
    angle = (
        2.0 * jnp.pi * (inner_ids[:, None] * half_ids[None, :] % inner).astype(jnp.float32) / inner
    )
    cos, sin = jnp.cos(angle), jnp.sin(angle)
    forward = jnp.concatenate(
        [jnp.concatenate([cos, -sin], 1), jnp.concatenate([sin, cos], 1)], 0
    )
    backward = jnp.concatenate(
        [jnp.concatenate([cos.T, sin.T], 1), jnp.concatenate([-sin.T, cos.T], 1)], 0
    ) * (2.0 / length)
    return (
        spread(jnp.cos(twist)),
        spread(jnp.sin(twist)),
        *split_table(forward),
        *split_table(backward),
    )


def stencil_kernel(
    share,
    state_ref, state_prev_ref, state_next_ref,
    pre_ref, pre_prev_ref, pre_next_ref, pre_first_ref, pre_last_ref,
    kappa_ref, column_ref, row_ref,
    *rest,
):
    pre_out_ref, jac_out_ref, side_ref = rest[-3:]
    i = pl.program_id(0)
    last = pl.num_programs(0) - 1
    width = state_ref.shape[2]
    strips = share // 8
    nudge = 0.25 * step_size

    def flux(low, high):
        total = low + high
        return (1.0 + total * total) * (high - low)

    lane = lax.broadcasted_iota(jnp.int32, (8, width), 1)
    sub = lax.broadcasted_iota(jnp.int32, (8, width), 0)

    table = jnp.transpose(column_ref[0], (1, 0))
    halo = jnp.transpose(pre_ref[0, share : share + 8, :128], (1, 0))
    side_ref[0, :, :8] = table
    side_ref[1, :, :8] = halo

    state_south = jnp.where(i == 0, row_ref[0:1, :], state_prev_ref[0, 7:8, :]) * 0.25
    state_north = jnp.where(i == last, row_ref[1:2, :], state_next_ref[0, 0:1, :]) * 0.25
    pre_south = jnp.where(i == 0, pre_last_ref[0, 3:4, :], pre_prev_ref[0, 7:8, :])
    pre_north = jnp.where(i == last, pre_first_ref[0, 2:3, :], pre_next_ref[0, 0:1, :])
    moved_south = state_south + pre_south * nudge
    moved_north = state_north + pre_north * nudge

    def load(g):
        rows = slice(g * 8, g * 8 + 8)
        state, pre = state_ref[0, rows, :] * 0.25, pre_ref[0, rows, :]
        return state, pre, state + pre * nudge

    here = load(0)
    below = flux(moved_south, here[2][:1]) - flux(state_south, here[0][:1])
    for g in range(strips):
        rows = slice(g * 8, g * 8 + 8)
        state, pre, moved = here
        if g + 1 < strips:
            here = load(g + 1)
            state_up, moved_up = here[0][:1], here[2][:1]
        else:
            state_up, moved_up = state_north, moved_north
        edge = lambda k: side_ref[0, rows, k : k + 1]
        zonal, north_factor, south_factor = edge(2), edge(3), edge(4)
        state_west, state_east = edge(0), edge(1)
        moved_west = state_west + side_ref[1, rows, 0:1] * nudge
        moved_east = state_east + side_ref[1, rows, 1:2] * nudge

        def from_east(field, column):
            return jnp.where(lane == width - 1, column, pltpu.roll(field, width - 1, 1))

        east = flux(moved, from_east(moved, moved_east)) - flux(state, from_east(state, state_east))
        west_edge = flux(moved_west, moved[:, :1]) - flux(state_west, state[:, :1])
        west = jnp.where(lane == 0, west_edge, pltpu.roll(east, 1, 1))
        spread = zonal * (east - west)

        def from_north(field, row):
            return pltpu.roll(jnp.where(sub == 0, row, field), 7, 0)

        north = flux(moved, from_north(moved, moved_up)) - flux(state, from_north(state, state_up))
        south = pltpu.roll(jnp.where(sub == 7, below, north), 1, 0)
        below = north[7:8]
        spread = spread + (north_factor * north - south_factor * south)
        pre_out_ref[0, rows, :] = pre
        jac_out_ref[0, rows, :] = pre - kappa_ref[rows, :].astype(jnp.float32) * spread


def stencil(level, state, pre, kappa, columns, rows, previous):
    _, row_count, width = state.shape
    steps = pre.shape[0]
    share = row_count // steps
    per = share // 8
    before = lambda i: jnp.maximum(i * per - 1, 0)
    after = lambda i: jnp.minimum((i + 1) * per, steps * per - 1)
    plane = pl.BlockSpec((1, share, width), lambda i: (level, i, 0))
    eight = lambda place: pl.BlockSpec((1, 8, width), place)
    in_specs = [
        plane,
        eight(lambda i: (level, before(i), 0)),
        eight(lambda i: (level, after(i), 0)),
        pl.BlockSpec((1, share + 8, width), lambda i: (i, 0, 0)),
        eight(lambda i: (jnp.maximum(i - 1, 0), per - 1, 0)),
        eight(lambda i: (jnp.minimum(i + 1, steps - 1), 0, 0)),
        eight(lambda i: (0, per, 0)),
        eight(lambda i: (steps - 1, per, 0)),
        pl.BlockSpec((share, width), lambda i: (i, 0)),
        pl.BlockSpec((1, 8, 128), lambda i: (i, 0, 0)),
        pl.BlockSpec((8, width), lambda i: (0, 0)),
    ]
    operands = [state, state, state, pre, pre, pre, pre, pre, kappa, columns, rows]
    aliases = {}
    if previous is not None:
        aliases = {len(operands): 0, len(operands) + 1: 1}
        operands += list(previous)
        in_specs += [pl.BlockSpec(memory_space=pl.ANY)] * 2
    shape = jax.ShapeDtypeStruct(state.shape, jnp.float32)
    return pl.pallas_call(
        functools.partial(stencil_kernel, share),
        grid=(steps,),
        in_specs=in_specs,
        out_specs=[plane, plane],
        out_shape=[shape, shape],
        scratch_shapes=[pltpu.VMEM((2, 128, 128), jnp.float32)],
        input_output_aliases=aliases,
        compiler_params=pltpu.CompilerParams(
            dimension_semantics=("arbitrary",), vmem_limit_bytes=12 * 1024 * 1024
        ),
        name="stencil",
    )(*operands)


def row_factors(first_row, count, total):
    rows = (first_row + jnp.arange(count, dtype=jnp.int32)).astype(jnp.float32)
    limit = jnp.float32(total)
    cell_cos = jnp.sin(jnp.pi * (rows + 0.5) / limit)
    high_face = rows + 1.0
    face_low = jnp.where((rows > 0.0) & (rows < limit), jnp.sin(jnp.pi * rows / limit), 0.0)
    face_high = jnp.where(high_face < limit, jnp.sin(jnp.pi * high_face / limit), 0.0)
    zonal_factor = jnp.minimum(1.0 / (cell_cos * cell_cos), zonal_cap)
    scale = 4.0 / step_size
    return (
        scale * zonal_tau * zonal_factor,
        scale * merid_tau * face_high / cell_cos,
        scale * merid_tau * face_low / cell_cos,
    )


def shifted(block, axis):
    count = lax.axis_size(axis)
    return lax.ppermute(block, axis, [(i, (i + 1) % count) for i in range(count)])


def shifted_back(block, axis):
    count = lax.axis_size(axis)
    return lax.ppermute(block, axis, [((i + 1) % count, i) for i in range(count)])


def exchange(block):
    return lax.all_to_all(block, "lon", 0, 0, tiled=True)


def on_device(state, direction, diffusivity, inverses):
    levels, local_rows, width = state.shape
    bands = lax.axis_size("lat")
    lons = lax.axis_size("lon")
    outer = inverses.shape[3]
    inner = 2 * inverses.shape[4]
    share = local_rows // lons
    step_rows = math.gcd(share, 48)

    pencils = []
    for level in range(levels):
        source = direction if level == 0 else lax.optimization_barrier(direction)
        pencils.append(source[level].reshape(lons, share, width))
    pencils = [exchange(pencil) for pencil in pencils]

    tables = transform_tables(outer, inner)
    arranged = jnp.transpose(inverses, (0, 3, 2, 1, 4))

    state_south = shifted(state[:, -1, :], "lat")
    state_north = shifted_back(state[:, 0, :], "lat")
    state_west = shifted(state[:, :, -1], "lon") * 0.25
    state_east = shifted_back(state[:, :, 0], "lon") * 0.25
    factors = row_factors(lax.axis_index("lat") * local_rows, local_rows, bands * local_rows)
    columns, rows = [], []
    for level in range(levels):
        lanes = jnp.stack([state_west[level], state_east[level], *factors], 0)
        lanes = jnp.transpose(lanes.reshape(-1, lons, share), (1, 0, 2))
        columns.append(jnp.pad(lanes, ((0, 0), (0, 8 - lanes.shape[1]), (0, 128 - share))))
        pair = jnp.stack([state_south[level], state_north[level]], 0)
        rows.append(jnp.pad(pair, ((0, 6), (0, 0))))

    fields = []
    for level in range(levels):
        block = spectral(pencils[level], arranged, tables, step_rows)
        north = shifted_back(block[:, 0, :], "lat")
        south = shifted(block[:, share - 1, :], "lat")
        block = block.at[:, share + 2 : share + 4, :].set(jnp.stack([north, south], 1))
        fields.append(exchange(block))

    outputs = None
    for level in range(levels):
        outputs = stencil(
            level, state, fields[level], diffusivity, columns[level], rows[level], outputs
        )
    return tuple(outputs)


def solution(mesh):
    return jax.shard_map(
        on_device,
        mesh=mesh,
        in_specs=(
            P(None, "lat", "lon"),
            P(None, "lat", "lon"),
            P("lat", "lon"),
            P(("lat", "lon"), None, None, None, None),
        ),
        out_specs=(P(None, "lat", "lon"), P(None, "lat", "lon")),
        check_vma=False,
    )
```

time: 361 us -> 188 us (0.52)
  matrix products: 85.6 us -> 0 us
  other arithmetic: 74.9 us -> 10.4 us
  Pallas kernels: 0 us -> 49.2 us
  waiting for transfers between devices: 99.4 us -> 52.7 us
  local copies, waits for them, and re-layouts: 69.9 us -> 41.9 us
  starting transfers between devices: 24.8 us -> 31.7 us
    dot_general x6 -> x0, matrix products: 85.6 us -> none  [the longest x4 43.9 us: batch_apply(): lax.dot_general(wide, values, (((2,), (1,)), ((0,), (0,))), precision=hig...]
    all_to_all x2 -> x4, waiting for transfers between devices: 99.4 us -> 28.1 us  [exchange(): return lax.all_to_all(block, 'lon', 0, 0, tiled=True)]
    pallas_call x0 -> x4, Pallas kernels: none -> 49.2 us  [the longest x2 27.6 us: spectral(): pl.pallas_call(functools.partial(spectral_kernel, outer, inner, step_rows...]
    ppermute x8, waiting for transfers between devices: 0.02 us -> 24.7 us  [the longest x4 24.7 us: shifted(): lax.ppermute(block, axis, [(i, (i + 1) % count) for i in range(count)])]
    div x2 -> x1, other arithmetic: 23.6 us -> 0.36 us  [row_factors(): scale * merid_tau * face_high / cell_cos]
    reshape x3 -> x0, local copies, waits for them, and re-layouts: 23.2 us -> none  [the longest x2 15.9 us: solve_rows(): return values.reshape(items, row_count, length)]
    unnamed x53 -> x46, local copies, waits for them, and re-layouts: 12.1 us -> 31 us
    all_to_all x2 -> x0, local copies, waits for them, and re-layouts: 17.1 us -> none  [the longest x1 9.8 us: spectral(): lax.all_to_all(values, 'lon', split_axis=2, concat_axis=1, tiled=True)]
  transfers between devices with their start and end apart: 10 -> 12, of which waited for: 2 -> 5; matrix products, arithmetic and copies ran while one was open for 12% -> 14% of each run, Pallas kernels for 0% -> 21%
where the time goes in v1:
time: 188 us; the launch traced here: 187 us
  waiting for transfers between devices  52.7 us (28%)
  Pallas kernels  49.2 us (26%)
  local copies, waits for them, and re-layouts  41.9 us (22%)
  starting transfers between devices  31.7 us (17%)
  other arithmetic  10.4 us (6%)
    unnamed x46, local copies, waits for them, and re-layouts  31 us
    all_to_all x4, waiting for transfers between devices, exchange(): return lax.all_to_all(block, 'lon', 0, 0, tiled=True)  28.1 us
    pallas_call x2, Pallas kernels, spectral(): pl.pallas_call(functools.partial(spectral_kernel, outer, inner, step_rows...  27.6 us
    ppermute x4, waiting for transfers between devices, shifted(): lax.ppermute(block, axis, [(i, (i + 1) % count) for i in range(count)])  24.7 us
    pallas_call x2, Pallas kernels, stencil(): pl.pallas_call(functools.partial(stencil_kernel, share), grid=(steps,), i...  21.6 us
    all_to_all x4, starting transfers between devices, exchange(): return lax.all_to_all(block, 'lon', 0, 0, tiled=True)  17.2 us
    ppermute x4, starting transfers between devices, shifted_back(): lax.ppermute(block, axis, [((i + 1) % count, i) for i in range(count)])  11.1 us
    slice x2, local copies, waits for them, and re-layouts, on_device(): pencils.append(source[level].reshape(lons, share, width))  6.48 us
  transfers between devices with their start and end apart: 12, of which 5 were waited for; matrix products, arithmetic and copies ran while one was open for 14% of the time, Pallas kernels for 21%

profile of v1, /device:TPU:0, one launch (start us, length us, event | category | flops | bytes accessed | tf_op | source)
XLA Modules:
  0.0 186.8 jit_solution(2658434984041419745)
XLA Ops:
  0.6 3.2 %slice.109 = f32[1,768,768]{2,1,0:T(8,128)} slice(f32[2,768,768]{2,1,0:T(8,128)} %param.9), slice={[0:1], [0:768], [0:768]} | slice | bytes 4718592 | tf_op jit(solution)/shard_map/slice | solution.py:434
  3.9 5.2 %all-to-all-start.2 = ((f32[8,96,768]{2,1,0:T(8,128)}), f32[8,96,768]{2,1,0:T(8,128)S(1)}, u32[]{:S(2)}, u32[]{:S(2)}) async-start(f32[8,96,768]{2,1,0:T(8,128)} %bitcast.30), calls=%async_computation.2 | async-start | bytes 4718592 | tf_op jit(solution)/shard_map/all_to_all | solution.py:419
  9.1 3.3 %slice.116 = f32[1,768,768]{2,1,0:T(8,128)} slice(f32[2,768,768]{2,1,0:T(8,128)} %param.9), slice={[1:2], [0:768], [0:768]} | slice | bytes 4718592 | tf_op jit(solution)/shard_map/slice | solution.py:434
  12.3 26.2 %all-to-all-done.2.y_ref = f32[8,96,768]{2,1,0:T(8,128)S(1)} async-done(((f32[8,96,768]{2,1,0:T(8,128)}), f32[8,96,768]{2,1,0:T(8,128)S(1)}, u32[]{:S(2)}, u32[]{:S(2)}) %all-to-all-start.2) | async-done | bytes 2359328 | tf_op jit(solution)/shard_map/all_to_all | solution.py:419
  38.5 1.4 copy-done.15
  39.9 4.4 %all-to-all-start = ((f32[8,96,768]{2,1,0:T(8,128)}), f32[8,96,768]{2,1,0:T(8,128)}, u32[]{:S(2)}, u32[]{:S(2)}) async-start(f32[8,96,768]{2,1,0:T(8,128)} %bitcast.29), calls=%async_computation | async-start | bytes 4718592 | tf_op jit(solution)/shard_map/all_to_all | solution.py:419
  44.2 7.5 %copy.48 = bf16[12,8,8,12,256]{4,1,2,3,0:T(8,128)(2,1)S(1)} copy(bf16[12,8,8,12,256]{4,2,3,1,0:T(8,128)(2,1)} %param.11) | data formatting | bytes 9437184 | tf_op args[3]
  52.1 1.9 %fusion.19 = f32[256,512]{1,0:T(8,128)S(1)} fusion(), kind=kLoop, calls=%fused_computation.33 | loop fusion | flops 1966080 | bytes 524288 | tf_op jit(solution)/shard_map/neg | solution.py:265
  54.0 1.9 %fusion.18 = f32[512,256]{1,0:T(8,128)S(1)} fusion(), kind=kLoop, calls=%fused_computation.32 | loop fusion | flops 1966080 | bytes 524288 | tf_op jit(solution)/shard_map/neg | solution.py:262
  56.0 2.2 %fusion.16 = (f32[512,256]{1,0:T(8,128)S(1)}, f32[512,256]{1,0:T(8,128)S(1)}) fusion(), kind=kLoop, calls=%fused_computation.30 | loop fusion | flops 1835008 | bytes 1048576 | tf_op jit(solution)/shard_map/sin | solution.py:260
  58.2 2.1 %fusion.14 = (f32[256,512]{1,0:T(8,128)S(1)}, f32[256,512]{1,0:T(8,128)S(1)}) fusion(), kind=kLoop, calls=%fused_computation.28 | loop fusion | flops 1835008 | bytes 1048576 | tf_op jit(solution)/shard_map/sin | solution.py:260
  60.3 0.3 fusion
  60.7 0.4 fusion.1
  61.2 2.6 %copy-done.16 = f32[8,96,768]{2,1,0:T(8,128)S(1)} copy-done((f32[8,96,768]{2,1,0:T(8,128)S(1)}, f32[8,96,768]{2,1,0:T(8,128)}, u32[]{:S(2)}) %copy-start.16) | copy-done | bytes 2359320
  63.8 12.7 %spectral.3 = f32[8,104,768]{2,1,0:T(8,128)S(1)} custom-call(f32[8,96,768]{2,1,0:T(8,128)S(1)} %copy-done.16, bf16[12,12,8,8,256]{4,3,2,1,0:T(8,128)(2,1)S(1)} %bitcast.27, f32[12,8,512]{2,1,0:T(8,128)S(1)} %broadcast_in_dim.12.tc_ref, f32[12,8,512]{2,1,0:T(8,128)S(1)} %broadcast_in_dim.26.ts_ref, bf16[1024,512]{1,0:T(8,128)(2,1)S(1)} %get-tuple-element.45.fh_ref, ...), custom_call_target="tpu_custom_call" | custom-call | tf_op jit(solution)/shard_map/spectral/pallas_call | solution.py:216
  76.6 1.6 collective-permute-start.7
  78.2 2.2 %collective-permute-start.6 = (f32[8,768]{1,0:T(8,128)S(1)}, f32[8,768]{1,0:T(8,128)S(1)}, u32[]{:S(2)}, u32[]{:S(2)}) collective-permute-start(f32[8,768]{1,0:T(8,128)S(1)} %bitcast.33), channel_id=1, source_target_pairs={{8,0},{16,8},{24,16},{0,24},{9,1},{17,9},{25,17},{1,25},{10,2},{18... | collective-permute-start | bytes 73736 | tf_op jit(solution)/shard_map/ppermute | solution.py:415
  80.5 1.9 %collective-permute-done.7 = f32[8,768]{1,0:T(8,128)S(1)} collective-permute-done((f32[8,768]{1,0:T(8,128)S(1)}, f32[8,768]{1,0:T(8,128)S(1)}, u32[]{:S(2)}, u32[]{:S(2)}) %collective-permute-start.7) | collective-permute-done | bytes 24608 | tf_op jit(solution)/shard_map/ppermute | solution.py:410
  82.5 1.5 copy-done.6
  84.0 4.0 %all-to-all-start.3 = ((f32[8,104,768]{2,1,0:T(8,128)}), f32[8,104,768]{2,1,0:T(8,128)S(1)}, u32[]{:S(2)}, u32[]{:S(2)}) async-start(f32[8,104,768]{2,1,0:T(8,128)} %copy-done.6), calls=%async_computation.3 | async-start | bytes 5111808 | tf_op jit(solution)/shard_map/all_to_all | solution.py:419
  88.0 2.3 %copy-done.5 = bf16[12,8,8,12,256]{4,1,2,3,0:T(8,128)(2,1)S(1)} copy-done((bf16[12,8,8,12,256]{4,1,2,3,0:T(8,128)(2,1)S(1)}, bf16[12,8,8,12,256]{4,1,2,3,0:T(8,128)(2,1)}, u32[]{:S(2)}) %copy-start.5) | copy-done | bytes 4718616
  90.4 1.2 copy-done.8
  91.6 1.2 copy-done.10
  92.8 1.2 copy-done.12
  94.1 1.2 copy-done.14
  95.3 14.9 %spectral.2 = f32[8,104,768]{2,1,0:T(8,128)} custom-call(f32[8,96,768]{2,1,0:T(8,128)} %all-to-all-done.y_ref, bf16[12,12,8,8,256]{4,3,2,1,0:T(8,128)(2,1)S(1)} %bitcast.28, f32[12,8,512]{2,1,0:T(8,128)S(1)} %broadcast_in_dim.12.tc_ref, f32[12,8,512]{2,1,0:T(8,128)S(1)} %broadcast_in_dim.26.ts_ref, bf16[1024,512]{1,0:T(8,128)(2,1)S(1)} %copy-done.10, ...), custom_call_target="tpu_custom_call" | custom-call | tf_op jit(solution)/shard_map/spectral/pallas_call | solution.py:216
  110.2 1.1 fusion.31
  111.3 1.3 collective-permute-start.1
  112.6 2.5 %collective-permute-start = (f32[8,768]{1,0:T(8,128)S(1)}, f32[8,768]{1,0:T(8,128)S(1)}, u32[]{:S(2)}, u32[]{:S(2)}) collective-permute-start(f32[8,768]{1,0:T(8,128)S(1)} %bitcast.34), channel_id=1, source_target_pairs={{8,0},{16,8},{24,16},{0,24},{9,1},{17,9},{25,17},{1,25},{10,2},{18... | collective-permute-start | bytes 73736 | tf_op jit(solution)/shard_map/ppermute | solution.py:415
  115.1 1.8 collective-permute-done.1
  117.0 0.7 maximum_dynamic-update-slice_fusion
  117.7 1.9 %all-to-all-done.3.pre_ref.pre_prev_ref.pre_next_ref.pre_first_ref.pre_last_ref = f32[8,104,768]{2,1,0:T(8,128)S(1)} async-done(((f32[8,104,768]{2,1,0:T(8,128)}), f32[8,104,768]{2,1,0:T(8,128)S(1)}, u32[]{:S(2)}, u32[]{:S(2)}) %all-to-all-start.3) | async-done | bytes 2555936 | tf_op jit(solution)/shard_map/all_to_all | solution.py:419
  119.6 1.5 copy-done.2
  121.0 3.6 %all-to-all-start.1 = ((f32[8,104,768]{2,1,0:T(8,128)}), f32[8,104,768]{2,1,0:T(8,128)S(1)}, u32[]{:S(2)}, u32[]{:S(2)}) async-start(f32[8,104,768]{2,1,0:T(8,128)} %maximum_dynamic-update-slice_fusion), calls=%async_computation.1 | async-start | bytes 5111808 | tf_op jit(solution)/shard_map/all_to_all | solution.py:419
  124.7 0.8 fusion.29
  125.5 3.8 %collective-permute-start.5 = (f32[2,768]{1,0:T(2,128)S(1)}, f32[2,768]{1,0:T(2,128)S(1)}, u32[]{:S(2)}, u32[]{:S(2)}) collective-permute-start(f32[2,768]{1,0:T(2,128)S(1)} %bitcast.40), channel_id=1, source_target_pairs={{8,0},{16,8},{24,16},{0,24},{9,1},{17,9},{25,17},{1,25},{10,2},{18... | collective-permute-start | bytes 18440 | tf_op jit(solution)/shard_map/ppermute | solution.py:415
  129.3 1.9 %slice_reduce_fusion = (f32[2,768]{1,0:T(2,128)S(1)}, f32[2,768,1]{2,1,0:T(8,128)S(1)}) fusion(f32[2,768,768]{2,1,0:T(8,128)} %state_next_ref.3), kind=kLoop, calls=%fused_computation.9 | loop fusion | bytes 24576 | tf_op jit(solution)/shard_map/slice | solution.py:443
  131.5 0.4 collective-permute-start.2
  131.8 2.5 %collective-permute-start.3 = (f32[2,768]{1,0:T(2,128)S(1)}, f32[2,768]{1,0:T(2,128)S(1)}, u32[]{:S(2)}, u32[]{:S(2)}) collective-permute-start(f32[2,768]{1,0:T(2,128)S(1)} %get-tuple-element.36), channel_id=1, source_target_pairs={{1,0},{2,1},{3,2},{4,3},{5,4},{6,5},{7,6},{0,7},{9,8},{10,9},{11,1... | collective-permute-start | bytes 18440 | tf_op jit(solution)/shard_map/ppermute | solution.py:415
  134.4 0.4 fusion.28
  134.8 20.9 %collective-permute-done.2 = f32[2,768]{1,0:T(2,128)S(1)} collective-permute-done((f32[2,768]{1,0:T(2,128)S(1)}, f32[2,768]{1,0:T(2,128)S(1)}, u32[]{:S(2)}, u32[]{:S(2)}) %collective-permute-start.2) | collective-permute-done | bytes 6176 | tf_op jit(solution)/shard_map/ppermute | solution.py:410
  156.3 2.3 %copy-done = f32[2,768,768]{2,1,0:T(8,128)S(1)} copy-done((f32[2,768,768]{2,1,0:T(8,128)S(1)}, f32[2,768,768]{2,1,0:T(8,128)}, u32[]{:S(2)}) %copy-start) | copy-done | bytes 4718616
  158.6 1.7 copy-done.3
  160.4 1.3 copy-done.17
  161.6 10.8 %stencil.2 = (f32[2,768,768]{2,1,0:T(8,128)}, f32[2,768,768]{2,1,0:T(8,128)}) custom-call(f32[2,768,768]{2,1,0:T(8,128)S(1)} %copy-done, f32[2,768,768]{2,1,0:T(8,128)S(1)} %copy-done, f32[2,768,768]{2,1,0:T(8,128)S(1)} %copy-done, f32[8,104,768]{2,1,0:T(8,128)S(1)} %copy-done.3, f32[8,104,768]{2,1,0:T(8,128)S(1)} %copy-done.3, ...), custom_call_target="tpu_custom_call" | custom-call | tf_op jit(solution)/shard_map/stencil/pallas_call | solution.py:377
  172.5 2.3 %copy-done.1 = f32[2,768,768]{2,1,0:T(8,128)S(1)} copy-done((f32[2,768,768]{2,1,0:T(8,128)S(1)}, f32[2,768,768]{2,1,0:T(8,128)}, u32[]{:S(2)}) %copy-start.1) | copy-done | bytes 4718616
  174.8 1.3 copy-done.18
  176.1 10.8 %stencil.3 = (f32[2,768,768]{2,1,0:T(8,128)}, f32[2,768,768]{2,1,0:T(8,128)}) custom-call(f32[2,768,768]{2,1,0:T(8,128)S(1)} %copy-done.1, f32[2,768,768]{2,1,0:T(8,128)S(1)} %copy-done.1, f32[2,768,768]{2,1,0:T(8,128)S(1)} %copy-done.1, ...), custom_call_target="tpu_custom_call", output_to_operand_aliasing={{0}: (11, {}), {1}: (12, {})} | custom-call | tf_op jit(solution)/shard_map/stencil/pallas_call | solution.py:377
  (66 shorter events, 1.4 us)
Async XLA Ops:
  3.9 34.6 %all-to-all-start.2 = ((f32[8,96,768]{2,1,0:T(8,128)}), f32[8,96,768]{2,1,0:T(8,128)S(1)}, u32[]{:S(2)}, u32[]{:S(2)}) async-start(f32[8,96,768]{2,1,0:T(8,128)} %bitcast.30), calls=%async_computation.2 | async-start | bytes 4718592 | tf_op jit(solution)/shard_map/all_to_all | solution.py:419
  38.5 1.4 copy-start.15
  39.9 44.1 %all-to-all-start = ((f32[8,96,768]{2,1,0:T(8,128)}), f32[8,96,768]{2,1,0:T(8,128)}, u32[]{:S(2)}, u32[]{:S(2)}) async-start(f32[8,96,768]{2,1,0:T(8,128)} %bitcast.29), calls=%async_computation | async-start | bytes 4718592 | tf_op jit(solution)/shard_map/all_to_all | solution.py:419
  51.8 9.4 %copy-start.4 = (bf16[12,8,8,12,256]{4,1,2,3,0:T(8,128)(2,1)}, bf16[12,8,8,12,256]{4,1,2,3,0:T(8,128)(2,1)S(1)}, u32[]{:S(2)}) copy-start(bf16[12,8,8,12,256]{4,1,2,3,0:T(8,128)(2,1)S(1)} %copy.48) | copy-start | bytes 14155780
  60.6 15.9 %copy-start.7 = (bf16[1024,512]{1,0:T(8,128)(2,1)}, bf16[1024,512]{1,0:T(8,128)(2,1)S(1)}, u32[]{:S(2)}) copy-start(bf16[1024,512]{1,0:T(8,128)(2,1)S(1)} %get-tuple-element.44.fl_ref) | copy-start | bytes 3145732
  60.6 15.9 %copy-start.9 = (bf16[1024,512]{1,0:T(8,128)(2,1)}, bf16[1024,512]{1,0:T(8,128)(2,1)S(1)}, u32[]{:S(2)}) copy-start(bf16[1024,512]{1,0:T(8,128)(2,1)S(1)} %get-tuple-element.45.fh_ref) | copy-start | bytes 3145732
  60.6 3.2 %copy-start.16 = (f32[8,96,768]{2,1,0:T(8,128)S(1)}, f32[8,96,768]{2,1,0:T(8,128)}, u32[]{:S(2)}) copy-start(f32[8,96,768]{2,1,0:T(8,128)} %copy-done.15) | copy-start | bytes 7077892
  61.1 15.4 %copy-start.11 = (bf16[512,1024]{1,0:T(8,128)(2,1)}, bf16[512,1024]{1,0:T(8,128)(2,1)S(1)}, u32[]{:S(2)}) copy-start(bf16[512,1024]{1,0:T(8,128)(2,1)S(1)} %get-tuple-element.42.gl_ref) | copy-start | bytes 3145732
  61.1 15.4 %copy-start.13 = (bf16[512,1024]{1,0:T(8,128)(2,1)}, bf16[512,1024]{1,0:T(8,128)(2,1)S(1)}, u32[]{:S(2)}) copy-start(bf16[512,1024]{1,0:T(8,128)(2,1)S(1)} %get-tuple-element.43.gh_ref) | copy-start | bytes 3145732
  76.6 5.8 %collective-permute-start.7 = (f32[8,768]{1,0:T(8,128)S(1)}, f32[8,768]{1,0:T(8,128)S(1)}, u32[]{:S(2)}, u32[]{:S(2)}) collective-permute-start(f32[8,768]{1,0:T(8,128)S(1)} %bitcast.35), channel_id=1, source_target_pairs={{0,8},{8,16},{16,24},{24,0},{1,9},{9,17},{17,25},{25,1},{2,10},{10... | collective-permute-start | bytes 73736 | tf_op jit(solution)/shard_map/ppermute | solution.py:410
  78.2 4.2 %collective-permute-start.6 = (f32[8,768]{1,0:T(8,128)S(1)}, f32[8,768]{1,0:T(8,128)S(1)}, u32[]{:S(2)}, u32[]{:S(2)}) collective-permute-start(f32[8,768]{1,0:T(8,128)S(1)} %bitcast.33), channel_id=1, source_target_pairs={{8,0},{16,8},{24,16},{0,24},{9,1},{17,9},{25,17},{1,25},{10,2},{18... | collective-permute-start | bytes 73736 | tf_op jit(solution)/shard_map/ppermute | solution.py:415
  82.5 1.5 copy-start.6
  84.0 35.6 %all-to-all-start.3 = ((f32[8,104,768]{2,1,0:T(8,128)}), f32[8,104,768]{2,1,0:T(8,128)S(1)}, u32[]{:S(2)}, u32[]{:S(2)}) async-start(f32[8,104,768]{2,1,0:T(8,128)} %copy-done.6), calls=%async_computation.3 | async-start | bytes 5111808 | tf_op jit(solution)/shard_map/all_to_all | solution.py:419
  88.0 2.3 %copy-start.5 = (bf16[12,8,8,12,256]{4,1,2,3,0:T(8,128)(2,1)S(1)}, bf16[12,8,8,12,256]{4,1,2,3,0:T(8,128)(2,1)}, u32[]{:S(2)}) copy-start(bf16[12,8,8,12,256]{4,1,2,3,0:T(8,128)(2,1)} %copy-done.4) | copy-start | bytes 14155780
  90.4 1.2 copy-start.8
  91.6 1.2 copy-start.10
  92.8 1.2 copy-start.12
  94.1 1.2 copy-start.14
  111.3 5.7 %collective-permute-start.1 = (f32[8,768]{1,0:T(8,128)S(1)}, f32[8,768]{1,0:T(8,128)S(1)}, u32[]{:S(2)}, u32[]{:S(2)}) collective-permute-start(f32[8,768]{1,0:T(8,128)S(1)} %bitcast.36), channel_id=1, source_target_pairs={{0,8},{8,16},{16,24},{24,0},{1,9},{9,17},{17,25},{25,1},{2,10},{10... | collective-permute-start | bytes 73736 | tf_op jit(solution)/shard_map/ppermute | solution.py:410
  112.6 4.4 %collective-permute-start = (f32[8,768]{1,0:T(8,128)S(1)}, f32[8,768]{1,0:T(8,128)S(1)}, u32[]{:S(2)}, u32[]{:S(2)}) collective-permute-start(f32[8,768]{1,0:T(8,128)S(1)} %bitcast.34), channel_id=1, source_target_pairs={{8,0},{16,8},{24,16},{0,24},{9,1},{17,9},{25,17},{1,25},{10,2},{18... | collective-permute-start | bytes 73736 | tf_op jit(solution)/shard_map/ppermute | solution.py:415
  119.6 1.5 copy-start.2
  121.0 51.4 %all-to-all-start.1 = ((f32[8,104,768]{2,1,0:T(8,128)}), f32[8,104,768]{2,1,0:T(8,128)S(1)}, u32[]{:S(2)}, u32[]{:S(2)}) async-start(f32[8,104,768]{2,1,0:T(8,128)} %maximum_dynamic-update-slice_fusion), calls=%async_computation.1 | async-start | bytes 5111808 | tf_op jit(solution)/shard_map/all_to_all | solution.py:419
  125.5 9.2 %collective-permute-start.5 = (f32[2,768]{1,0:T(2,128)S(1)}, f32[2,768]{1,0:T(2,128)S(1)}, u32[]{:S(2)}, u32[]{:S(2)}) collective-permute-start(f32[2,768]{1,0:T(2,128)S(1)} %bitcast.40), channel_id=1, source_target_pairs={{8,0},{16,8},{24,16},{0,24},{9,1},{17,9},{25,17},{1,25},{10,2},{18... | collective-permute-start | bytes 18440 | tf_op jit(solution)/shard_map/ppermute | solution.py:415
  129.3 26.9 %collective-permute-start.4 = (f32[2,768]{1,0:T(2,128)S(1)}, f32[2,768]{1,0:T(2,128)S(1)}, u32[]{:S(2)}, u32[]{:S(2)}) collective-permute-start(f32[2,768]{1,0:T(2,128)S(1)} %bitcast.39), channel_id=1, source_target_pairs={{0,8},{8,16},{16,24},{24,0},{1,9},{9,17},{17,25},{25,1},{2,10},{10... | collective-permute-start | bytes 18440 | tf_op jit(solution)/shard_map/ppermute | solution.py:410
  131.5 24.2 %collective-permute-start.2 = (f32[2,768]{1,0:T(2,128)S(1)}, f32[2,768]{1,0:T(2,128)S(1)}, u32[]{:S(2)}, u32[]{:S(2)}) collective-permute-start(f32[2,768]{1,0:T(2,128)S(1)} %bitcast.38), channel_id=1, source_target_pairs={{0,1},{1,2},{2,3},{3,4},{4,5},{5,6},{6,7},{7,0},{8,9},{9,10},{10,1... | collective-permute-start | bytes 18440 | tf_op jit(solution)/shard_map/ppermute | solution.py:410
  131.8 23.9 %collective-permute-start.3 = (f32[2,768]{1,0:T(2,128)S(1)}, f32[2,768]{1,0:T(2,128)S(1)}, u32[]{:S(2)}, u32[]{:S(2)}) collective-permute-start(f32[2,768]{1,0:T(2,128)S(1)} %get-tuple-element.36), channel_id=1, source_target_pairs={{1,0},{2,1},{3,2},{4,3},{5,4},{6,5},{7,6},{0,7},{9,8},{10,9},{11,1... | collective-permute-start | bytes 18440 | tf_op jit(solution)/shard_map/ppermute | solution.py:415
  156.3 2.3 %copy-start = (f32[2,768,768]{2,1,0:T(8,128)S(1)}, f32[2,768,768]{2,1,0:T(8,128)}, u32[]{:S(2)}) copy-start(f32[2,768,768]{2,1,0:T(8,128)} %state_next_ref.3) | copy-start | bytes 14155780
  158.6 1.7 copy-start.3
  160.4 1.3 copy-start.17
  172.5 2.3 %copy-start.1 = (f32[2,768,768]{2,1,0:T(8,128)S(1)}, f32[2,768,768]{2,1,0:T(8,128)}, u32[]{:S(2)}) copy-start(f32[2,768,768]{2,1,0:T(8,128)} %state_next_ref.3) | copy-start | bytes 14155780
  174.8 1.3 copy-start.18
